TPU v7x, 256 devices: a whole 4x4x8 slice. The times are simulated.
256 devices in a mesh: expert: 8 (over y, core), shard: 32 (over z, x).
Axes of the slice: x: 4, y: 4, z: 8, core: 2. Of those that a mesh axis runs over, the one named last changes fastest.
Arguments:
- master_down: float32 [16, 6400, 4096], P('expert', None, 'shard'), may hold values from -0.15625 to 0.15625
- second_down: bfloat16 [16, 6400, 4096], P('expert', None, 'shard'), may hold values from -0.0390625 to 0.0390625
- router_weight: float32 [4096, 16], P('shard', 'expert'), may hold values from -0.09375 to 0.09375
- router_gain: float32 [4096], P('shard'), may hold values from 0.25 to 1.75
Outputs:
- final_down: bfloat16 [16, 6400, 4096], P('expert', 'shard')
- scale_down: float32 [16, 6400], P('expert', 'shard')
- serve_router: bfloat16 [4096, 16], replicated
All inputs are finite; a program needn't handle non-finite values.
Results may differ from a plain program's by a relative error of at most 0.0085.
Values may be sent and summed in bfloat16 or wider, within the bound.
No kernel may reach another device: no remote copies, remote signals or barrier semaphores. Data moves between devices by JAX's collectives and lax.ppermute only.
A program may use at most 64 MiB of HBM per device.

v0:
```python
import jax
import jax.numpy as jnp
from jax import lax
from jax.sharding import PartitionSpec as P


def sent_to_all(x, axis):
    count = lax.axis_size(axis)
    return lax.all_to_all(jnp.broadcast_to(x[None], (count, *x.shape)), axis, 0, 0, tiled=True)


def taken_together(x, axis):
    everything = sent_to_all(x, axis)
    return jnp.sum(everything.astype(jnp.float32), axis=0)


def laid_out(parts, dim):
    dims = list(parts.shape[1:])
    dims[dim] *= parts.shape[0]
    return jnp.moveaxis(parts, 0, dim).reshape(dims)


def gathered_copies(x, axis, dim):
    parts = sent_to_all(x, axis)
    return laid_out(parts, dim)


def body(master_down, second_down, router_weight, router_gain):
    merged_down = master_down + second_down.astype(jnp.float32)
    total_down = taken_together(
        jnp.sum(merged_down * merged_down, axis=2).astype(jnp.bfloat16), "shard"
    ).astype(jnp.float32)
    scale_down = jnp.sqrt(total_down)
    narrow_down = (merged_down / jnp.expand_dims(scale_down, 2)).astype(jnp.bfloat16)
    final_down = lax.all_to_all(narrow_down, "shard", split_axis=1, concat_axis=2, tiled=True)
    scale_down = lax.dynamic_slice_in_dim(
        scale_down, lax.axis_index("shard") * final_down.shape[1], final_down.shape[1], axis=1
    )
    part_router = (router_weight * router_gain[:, None]).astype(jnp.bfloat16)
    row_router = gathered_copies(part_router, "shard", 0)
    serve_router = gathered_copies(row_router, "expert", 1)
    return (final_down, scale_down, serve_router)


def solution(mesh):
    placed = (
        P("expert", None, "shard"),
        P("expert", None, "shard"),
        P("shard", "expert"),
        P("shard"),
    )
    return jax.shard_map(
        body,
        mesh=mesh,
        in_specs=placed,
        out_specs=(P("expert", "shard", None), P("expert", "shard"), P()),
        check_vma=False,
    )
```

profile of v0, /device:TPU:3, one launch (start us, length us, event | category | flops | bytes accessed | tf_op | source)
XLA Modules:
  0.0 183.1 jit_solution(7028451042214102554)
XLA Ops:
  0.6 0.7 multiply_convert_fusion
  1.3 0.6 broadcast_in_dim.9
  1.9 11.1 %all-to-all-start.2 = ((bf16[32,128,2]{1,2,0:T(2,128)(2,1)}), bf16[32,128,2]{1,2,0:T(2,128)(2,1)S(1)}, u32[]{:S(2)}, u32[]{:S(2)}) async-start(bf16[32,128,2]{1,2,0:T(2,128)(2,1)} %broadcast_in_dim.9), calls=%async_computation.2 | async-start | bytes 32768 | tf_op jit(solution)/shard_map/all_to_all | solution.py:9
  13.0 0.0 copy-start
  13.0 5.7 %multiply_reduce_fusion = bf16[2,6400]{1,0:T(2,128)(2,1)S(1)} fusion(f32[2,6400,128]{2,1,0:T(8,128)} %param.4, bf16[2,6400,128]{2,1,0:T(8,128)(2,1)} %param.5), kind=kLoop, calls=%fused_computation.1 | loop fusion | flops 6540800 | bytes 9856000 | tf_op jit(solution)/shard_map/reduce_sum | solution.py:31
  18.8 1.8 %all-to-all-done.2 = bf16[32,128,2]{1,2,0:T(2,128)(2,1)S(1)} async-done(((bf16[32,128,2]{1,2,0:T(2,128)(2,1)}), bf16[32,128,2]{1,2,0:T(2,128)(2,1)S(1)}, u32[]{:S(2)}, u32[]{:S(2)}) %all-to-all-start.2) | async-done | bytes 16416 | tf_op jit(solution)/shard_map/all_to_all | solution.py:9
  20.6 0.4 broadcast_in_dim.8
  21.0 29.0 %all_to_all.33 = bf16[32,2,6400]{2,1,0:T(2,128)(2,1)} all-to-all(bf16[32,2,6400]{2,1,0:T(2,128)(2,1)S(1)} %broadcast_in_dim.8), channel_id=1, replica_groups=mesh['expert'=8,'shard'=32] {'shard'}, dimensions={0} | all-to-all | bytes 1638400 | tf_op jit(solution)/shard_map/all_to_all | solution.py:9
  50.1 0.7 broadcast_in_dim.11
  50.8 7.1 %all-to-all-start.3 = ((bf16[8,4096,2]{1,2,0:T(2,128)(2,1)}), bf16[8,4096,2]{1,2,0:T(2,128)(2,1)S(1)}, u32[]{:S(2)}, u32[]{:S(2)}) async-start(bf16[8,4096,2]{1,2,0:T(2,128)(2,1)} %broadcast_in_dim.11), calls=%async_computation.3 | async-start | bytes 262144 | tf_op jit(solution)/shard_map/all_to_all | solution.py:9
  57.9 1.3 convert_reduce_fusion
  59.2 0.1 sqrt.7
  59.3 0.0 copy-done
  59.3 4.7 %divide_convert_fusion = bf16[2,6400,128]{2,1,0:T(8,128)(2,1)S(1)} fusion(f32[2,6400,128]{2,1,0:T(8,128)} %param.4, bf16[2,6400,128]{2,1,0:T(8,128)(2,1)S(1)} %copy-done, f32[2,6400]{1,0:T(2,128)S(1)} %sqrt.7), kind=kLoop, calls=%fused_computation | loop fusion | flops 6553600 | bytes 13158400 | tf_op jit(solution)/shard_map/convert_element_type | solution.py:34
  64.1 27.9 %copy.31 = bf16[2,6400,128]{2,0,1:T(2,128)(2,1)} copy(bf16[2,6400,128]{2,1,0:T(8,128)(2,1)S(1)} %divide_convert_fusion) | data formatting | bytes 6553600 | tf_op jit(solution)/shard_map/convert_element_type | solution.py:34
  91.9 0.0 all-to-all-done.3
  91.9 5.0 %all-to-all-start.1 = ((bf16[2,6400,128]{2,0,1:T(2,128)(2,1)}), bf16[2,6400,128]{2,0,1:T(2,128)(2,1)S(1)}, u32[]{:S(2)}, u32[]{:S(2)}) async-start(bf16[2,6400,128]{2,0,1:T(2,128)(2,1)} %copy.31), calls=%async_computation.1 | async-start | bytes 6553600 | tf_op jit(solution)/shard_map/all_to_all | solution.py:35
  97.0 0.7 reshape.18
  97.7 0.7 constant_dynamic-slice_fusion
  98.3 76.1 %all-to-all-done.1 = bf16[2,6400,128]{2,0,1:T(2,128)(2,1)S(1)} async-done(((bf16[2,6400,128]{2,0,1:T(2,128)(2,1)}), bf16[2,6400,128]{2,0,1:T(2,128)(2,1)S(1)}, u32[]{:S(2)}, u32[]{:S(2)}) %all-to-all-start.1) | async-done | bytes 3276832 | tf_op jit(solution)/shard_map/all_to_all | solution.py:35
  174.4 2.5 %copy.32 = bf16[2,200,32,128]{3,2,1,0:T(8,128)(2,1)} copy(bf16[2,200,32,128]{3,0,1,2:T(2,128)(2,1)S(1)} %bitcast.9) | data formatting | bytes 6553600 | tf_op jit(solution)/shard_map/all_to_all | solution.py:35
  176.9 6.2 %all_to_all.26 = bf16[2,200,4096]{2,1,0:T(8,128)(2,1)} reshape(bf16[2,200,32,128]{3,2,1,0:T(8,128)(2,1)} %copy.32) | data formatting | bytes 6553600 | tf_op jit(solution)/shard_map/all_to_all | solution.py:35
Async XLA Ops:
  1.9 18.7 %all-to-all-start.2 = ((bf16[32,128,2]{1,2,0:T(2,128)(2,1)}), bf16[32,128,2]{1,2,0:T(2,128)(2,1)S(1)}, u32[]{:S(2)}, u32[]{:S(2)}) async-start(bf16[32,128,2]{1,2,0:T(2,128)(2,1)} %broadcast_in_dim.9), calls=%async_computation.2 | async-start | bytes 32768 | tf_op jit(solution)/shard_map/all_to_all | solution.py:9
  13.0 46.3 %copy-start = (bf16[2,6400,128]{2,1,0:T(8,128)(2,1)S(1)}, bf16[2,6400,128]{2,1,0:T(8,128)(2,1)}, u32[]{:S(2)}) copy-start(bf16[2,6400,128]{2,1,0:T(8,128)(2,1)} %param.5) | copy-start | bytes 9830404
  50.8 41.1 %all-to-all-start.3 = ((bf16[8,4096,2]{1,2,0:T(2,128)(2,1)}), bf16[8,4096,2]{1,2,0:T(2,128)(2,1)S(1)}, u32[]{:S(2)}, u32[]{:S(2)}) async-start(bf16[8,4096,2]{1,2,0:T(2,128)(2,1)} %broadcast_in_dim.11), calls=%async_computation.3 | async-start | bytes 262144 | tf_op jit(solution)/shard_map/all_to_all | solution.py:9
  91.9 82.5 %all-to-all-start.1 = ((bf16[2,6400,128]{2,0,1:T(2,128)(2,1)}), bf16[2,6400,128]{2,0,1:T(2,128)(2,1)S(1)}, u32[]{:S(2)}, u32[]{:S(2)}) async-start(bf16[2,6400,128]{2,0,1:T(2,128)(2,1)} %copy.31), calls=%async_computation.1 | async-start | bytes 6553600 | tf_op jit(solution)/shard_map/all_to_all | solution.py:35
where the time goes:
time: 184 us; the launch traced here: 183 us
  waiting for transfers between devices  77.9 us (42%)
  local copies, waits for them, and re-layouts  39.8 us (22%)
  blocking collectives  29 us (16%)
  starting transfers between devices  23.2 us (13%)
  other arithmetic  12.5 us (7%)
    all_to_all x1, waiting for transfers between devices, body(): lax.all_to_all(narrow_down, 'shard', split_axis=1, concat_axis=2, tiled=T...  76.1 us
    all_to_all x1, blocking collectives, sent_to_all(): lax.all_to_all(jnp.broadcast_to(x[None], (count, *x.shape)), axis, 0, 0,...  29 us
    convert_element_type x1, local copies, waits for them, and re-layouts, body(): (merged_down / jnp.expand_dims(scale_down, 2)).astype(jnp.bfloat16)  27.9 us
    all_to_all x2, starting transfers between devices, sent_to_all(): lax.all_to_all(jnp.broadcast_to(x[None], (count, *x.shape)), axis, 0, 0,...  18.2 us
    all_to_all x2, local copies, waits for them, and re-layouts, body(): lax.all_to_all(narrow_down, 'shard', split_axis=1, concat_axis=2, tiled=T...  8.72 us
    reduce_sum x1, other arithmetic, body(): jnp.sum(merged_down * merged_down, axis=2).astype(jnp.bfloat16)  5.75 us
    all_to_all x1, starting transfers between devices, body(): lax.all_to_all(narrow_down, 'shard', split_axis=1, concat_axis=2, tiled=T...  5.01 us
    convert_element_type x1, other arithmetic, body(): (merged_down / jnp.expand_dims(scale_down, 2)).astype(jnp.bfloat16)  4.74 us
  transfers between devices with their start and end apart: 3, of which 2 were waited for; matrix products, arithmetic and copies ran while one was open for 22% of the time, Pallas kernels for 0%

commit v1 on v0

--- a/solution.py
+++ b/solution.py
@@ -1,7 +1,20 @@
+import functools
 import jax
 import jax.numpy as jnp
 from jax import lax
 from jax.sharding import PartitionSpec as P
+
+
+def _step_on_pipes(x_in, chip_axis):
+    return jnp.concatenate(
+        lax.all_to_all(
+            jnp.stack(jnp.split(x_in, lax.axis_size(chip_axis), axis=1)), chip_axis, 0, 0
+        ),
+        axis=2,
+    )
+
+
+perform_gates = functools.partial(_step_on_pipes, chip_axis="shard")
 
 
 def sent_to_all(x, axis):
@@ -32,7 +45,7 @@
     ).astype(jnp.float32)
     scale_down = jnp.sqrt(total_down)
     narrow_down = (merged_down / jnp.expand_dims(scale_down, 2)).astype(jnp.bfloat16)
-    final_down = lax.all_to_all(narrow_down, "shard", split_axis=1, concat_axis=2, tiled=True)
+    final_down = perform_gates(narrow_down)
     scale_down = lax.dynamic_slice_in_dim(
         scale_down, lax.axis_index("shard") * final_down.shape[1], final_down.shape[1], axis=1
     )

time: 184 us -> 152 us (0.83)
  local copies, waits for them, and re-layouts: 39.8 us -> 7.59 us
    convert_element_type x1 -> x0, local copies, waits for them, and re-layouts: 27.9 us -> none  [body(): (merged_down / jnp.expand_dims(scale_down, 2)).astype(jnp.bfloat16)]
    all_to_all x2 -> x0, local copies, waits for them, and re-layouts: 8.72 us -> none  [body(): lax.all_to_all(narrow_down, 'shard', split_axis=1, concat_axis=2, tiled=T...]
    unnamed x2 -> x35, local copies, waits for them, and re-layouts: 0.01 us -> 2.25 us
    reshape x0 -> x1, local copies, waits for them, and re-layouts: none -> 2.14 us  [_step_on_pipes(): jnp.concatenate(lax.all_to_all(jnp.stack(jnp.split(x_in, lax.axis_size(ch...]
  transfers between devices with their start and end apart: 3 -> 3, of which waited for: 2 -> 2; matrix products, arithmetic and copies ran while one was open for 22% -> 9% of each run, Pallas kernels for 0% -> 0%
where the time goes in v1:
time: 152 us; the launch traced here: 151 us
  waiting for transfers between devices  78.1 us (51%)
  blocking collectives  29 us (19%)
  starting transfers between devices  23.2 us (15%)
  other arithmetic  12.4 us (8%)
  local copies, waits for them, and re-layouts  7.59 us (5%)
    all_to_all x1, waiting for transfers between devices, _step_on_pipes(): lax.all_to_all(jnp.stack(jnp.split(x_in, lax.axis_size(chip_axis), axis=1...  76.1 us
    all_to_all x1, blocking collectives, sent_to_all(): lax.all_to_all(jnp.broadcast_to(x[None], (count, *x.shape)), axis, 0, 0,...  29 us
    all_to_all x2, starting transfers between devices, sent_to_all(): lax.all_to_all(jnp.broadcast_to(x[None], (count, *x.shape)), axis, 0, 0,...  18.2 us
    reduce_sum x1, other arithmetic, body(): jnp.sum(merged_down * merged_down, axis=2).astype(jnp.bfloat16)  5.6 us
    all_to_all x1, starting transfers between devices, _step_on_pipes(): lax.all_to_all(jnp.stack(jnp.split(x_in, lax.axis_size(chip_axis), axis=1...  5.01 us
    convert_element_type x1, other arithmetic, body(): (merged_down / jnp.expand_dims(scale_down, 2)).astype(jnp.bfloat16)  4.74 us
  transfers between devices with their start and end apart: 3, of which 2 were waited for; matrix products, arithmetic and copies ran while one was open for 9% of the time, Pallas kernels for 0%

profile of v1, /device:TPU:3, one launch (start us, length us, event | category | flops | bytes accessed | tf_op | source)
XLA Modules:
  0.0 151.1 jit_solution(17886167564966132452)
XLA Ops:
  0.6 0.7 multiply_convert_fusion
  1.3 0.6 broadcast_in_dim.9
  1.9 11.1 %all-to-all-start.2 = ((bf16[32,128,2]{1,2,0:T(2,128)(2,1)}), bf16[32,128,2]{1,2,0:T(2,128)(2,1)S(1)}, u32[]{:S(2)}, u32[]{:S(2)}) async-start(bf16[32,128,2]{1,2,0:T(2,128)(2,1)} %broadcast_in_dim.9), calls=%async_computation.2 | async-start | bytes 32768 | tf_op jit(solution)/shard_map/all_to_all | solution.py:22
  13.0 5.6 %multiply_reduce_fusion = bf16[2,6400]{1,0:T(2,128)(2,1)S(1)} fusion(f32[2,6400,128]{2,1,0:T(8,128)} %param.4, bf16[2,6400,128]{2,1,0:T(8,128)(2,1)} %param.5), kind=kLoop, calls=%fused_computation.1 | loop fusion | flops 6540800 | bytes 9856000 | tf_op jit(solution)/shard_map/reduce_sum | solution.py:44
  18.6 0.0 copy-start
  18.6 2.0 %all-to-all-done.2 = bf16[32,128,2]{1,2,0:T(2,128)(2,1)S(1)} async-done(((bf16[32,128,2]{1,2,0:T(2,128)(2,1)}), bf16[32,128,2]{1,2,0:T(2,128)(2,1)S(1)}, u32[]{:S(2)}, u32[]{:S(2)}) %all-to-all-start.2) | async-done | bytes 16416 | tf_op jit(solution)/shard_map/all_to_all | solution.py:22
  20.6 0.4 broadcast_in_dim.8
  21.0 29.0 %all_to_all.20 = bf16[32,2,6400]{2,1,0:T(2,128)(2,1)} all-to-all(bf16[32,2,6400]{2,1,0:T(2,128)(2,1)S(1)} %broadcast_in_dim.8), channel_id=1, replica_groups=mesh['expert'=8,'shard'=32] {'shard'}, dimensions={0} | all-to-all | bytes 1638400 | tf_op jit(solution)/shard_map/all_to_all | solution.py:22
  50.0 0.7 broadcast_in_dim.11
  50.8 7.1 %all-to-all-start.3 = ((bf16[8,4096,2]{1,2,0:T(2,128)(2,1)}), bf16[8,4096,2]{1,2,0:T(2,128)(2,1)S(1)}, u32[]{:S(2)}, u32[]{:S(2)}) async-start(bf16[8,4096,2]{1,2,0:T(2,128)(2,1)} %broadcast_in_dim.11), calls=%async_computation.3 | async-start | bytes 262144 | tf_op jit(solution)/shard_map/all_to_all | solution.py:22
  57.9 1.3 convert_reduce_fusion
  59.2 0.1 sqrt.7
  59.3 0.0 copy-done
  59.3 4.7 %divide_convert_fusion = bf16[2,6400,128]{2,1,0:T(8,128)(2,1)S(1)} fusion(f32[2,6400,128]{2,1,0:T(8,128)} %param.4, bf16[2,6400,128]{2,1,0:T(8,128)(2,1)S(1)} %copy-done, f32[2,6400]{1,0:T(2,128)S(1)} %sqrt.7), kind=kLoop, calls=%fused_computation | loop fusion | flops 6553600 | bytes 13158400 | tf_op jit(solution)/shard_map/convert_element_type | solution.py:47
  64.8 0.0 copy-start.1
  64.8 1.7 %copy-done.1 = bf16[32,2,200,128]{3,2,1,0:T(8,128)(2,1)} copy-done((bf16[32,2,200,128]{3,2,1,0:T(8,128)(2,1)}, bf16[32,2,200,128]{3,2,1,0:T(8,128)(2,1)S(1)}, u32[]{:S(2)}) %copy-start.1) | copy-done | bytes 3276824
  66.5 0.0 all-to-all-done.3
  66.5 5.0 %all-to-all-start.1 = ((bf16[32,2,200,128]{3,2,1,0:T(8,128)(2,1)}), bf16[32,2,200,128]{3,2,1,0:T(8,128)(2,1)S(1)}, u32[]{:S(2)}, u32[]{:S(2)}) async-start(bf16[32,2,200,128]{3,2,1,0:T(8,128)(2,1)} %copy-done.1), calls=%async_computation.1 | async-start | bytes 6553600 | tf_op jit(solution)/shard_map/all_to_all | solution.py:10
  71.5 0.7 reshape.26
  72.3 0.7 constant_dynamic-slice_fusion
  72.9 76.1 %all-to-all-done.1 = bf16[32,2,200,128]{3,2,1,0:T(8,128)(2,1)S(1)} async-done(((bf16[32,2,200,128]{3,2,1,0:T(8,128)(2,1)}), bf16[32,2,200,128]{3,2,1,0:T(8,128)(2,1)S(1)}, u32[]{:S(2)}, u32[]{:S(2)}) %all-to-all-start.1) | async-done | bytes 3276832 | tf_op jit(solution)/shard_map/all_to_all | solution.py:10
  149.0 2.1 %copy_bitcast_fusion = bf16[2,200,4096]{2,1,0:T(8,128)(2,1)} fusion(bf16[32,2,200,128]{3,2,1,0:T(8,128)(2,1)S(1)} %all-to-all-done.1), kind=kLoop, calls=%fused_computation.3 | loop fusion | bytes 6553600 | tf_op jit(solution)/shard_map/reshape | solution.py:9
  (32 shorter events, 0.6 us)
Async XLA Ops:
  1.9 18.7 %all-to-all-start.2 = ((bf16[32,128,2]{1,2,0:T(2,128)(2,1)}), bf16[32,128,2]{1,2,0:T(2,128)(2,1)S(1)}, u32[]{:S(2)}, u32[]{:S(2)}) async-start(bf16[32,128,2]{1,2,0:T(2,128)(2,1)} %broadcast_in_dim.9), calls=%async_computation.2 | async-start | bytes 32768 | tf_op jit(solution)/shard_map/all_to_all | solution.py:22
  18.6 40.7 %copy-start = (bf16[2,6400,128]{2,1,0:T(8,128)(2,1)S(1)}, bf16[2,6400,128]{2,1,0:T(8,128)(2,1)}, u32[]{:S(2)}) copy-start(bf16[2,6400,128]{2,1,0:T(8,128)(2,1)} %param.5) | copy-start | bytes 9830404
  50.8 15.8 %all-to-all-start.3 = ((bf16[8,4096,2]{1,2,0:T(2,128)(2,1)}), bf16[8,4096,2]{1,2,0:T(2,128)(2,1)S(1)}, u32[]{:S(2)}, u32[]{:S(2)}) async-start(bf16[8,4096,2]{1,2,0:T(2,128)(2,1)} %broadcast_in_dim.11), calls=%async_computation.3 | async-start | bytes 262144 | tf_op jit(solution)/shard_map/all_to_all | solution.py:22
  64.8 1.7 %copy-start.1 = (bf16[32,2,200,128]{3,2,1,0:T(8,128)(2,1)}, bf16[32,2,200,128]{3,2,1,0:T(8,128)(2,1)S(1)}, u32[]{:S(2)}) copy-start(bf16[32,2,200,128]{3,2,1,0:T(8,128)(2,1)S(1)} %fusion) | copy-start | bytes 9830404
  66.5 82.5 %all-to-all-start.1 = ((bf16[32,2,200,128]{3,2,1,0:T(8,128)(2,1)}), bf16[32,2,200,128]{3,2,1,0:T(8,128)(2,1)S(1)}, u32[]{:S(2)}, u32[]{:S(2)}) async-start(bf16[32,2,200,128]{3,2,1,0:T(8,128)(2,1)} %copy-done.1), calls=%async_computation.1 | async-start | bytes 6553600 | tf_op jit(solution)/shard_map/all_to_all | solution.py:10
